TPU v7x, 32 devices: a whole 2x2x4 slice. The times are simulated.
32 devices in a mesh: src: 8 (over z, x), dst: 4 (over y, core).
Axes of the slice: x: 2, y: 2, z: 4, core: 2. Of those that a mesh axis runs over, the one named last changes fastest.
Arguments:
- counts: int32 [8, 2048, 4096], P(None, 'src', 'dst'), may hold values from 0 to 63
- src_factor: float32 [2048, 128], P('src'), may hold values from 0.25 to 32
- dst_factor: float32 [4096, 128], P('dst'), may hold values from 0.25 to 32
- hour_factor: float32 [8, 32], replicated, may hold values from 0.25 to 4
- core: float32 [32, 128, 128], replicated, may hold values from 1e-06 to 1e-05
Outputs:
- grad_src: float32 [2048, 128], P('src')
- grad_dst: float32 [4096, 128], P('dst')
- grad_hour: float32 [8, 32], replicated
- grad_core: float32 [32, 128, 128], P(None, 'src')
All inputs are finite; a program needn't handle non-finite values.
Results may differ from a plain program's by a relative error of at most 0.0003.
Values sent between devices are 32-bit elements; how exact they have to be, the bound alone decides.
A program may use at most 64 MiB of HBM per device.

v0:
```python
import functools
import math

import jax
import jax.numpy as jnp
from jax import lax
from jax.experimental import pallas as pl
from jax.experimental.pallas import tpu as pltpu
from jax.sharding import PartitionSpec as P

F32 = jnp.float32
BF16 = jnp.bfloat16
MESH = pl.DeviceIdType.MESH


def split(x):
    hi = x.astype(BF16)
    lo = (x - hi.astype(F32)).astype(BF16)
    return hi, lo


def dg(a, b, ca, cb):
    return lax.dot_general(a, b, (((ca,), (cb,)), ((), ())), preferred_element_type=F32)


def dot3(a, b, ca, cb):
    ah, al = a
    bh, bl = b
    return dg(ah, bh, ca, cb) + dg(ah, bl, ca, cb) + dg(al, bh, ca, cb)


def kernel(
    n, nz, nx, nd, tj,
    counts, src, dst, hour, core,
    g_src, g_dst, g_hour, g_core,
    cnt, ch, pf_ks, pf_t, d_k, d_n, thr, dacc, r1, r2,
    chs, gterm, r3, proj, q1, q2, pq, q3, pk, hacc, hd, hs,
    c_sem, s1s, s1r, s2s, s2r, zs, zr, xs, xr,
    gs1s, gs1r, gs2s, gs2r, q1s, q1r, q2s, q2r, q3s, q3r, pks, pkr, hds, hdr, hss, hsr,
):
    s = lax.axis_index("src")
    d = lax.axis_index("dst")
    a = s // nx
    b = lax.rem(s, nx)
    yy = d // 2
    cc = lax.rem(d, 2)
    ny = nd // 2
    kk, ni, _ = counts.shape
    nj = dst.shape[0]
    r3n = core.shape[0]
    r1n = core.shape[1]
    rows = nj // n
    half = nj // nx
    nb = half // tj
    cps = tj // rows
    kd = kk // nd
    share = r1n // n
    irows = ni // nd
    scale_src = 1.0 / math.sqrt(nj * nd * kk)
    scale_dst = 1.0 / math.sqrt(ni * n * kk)
    scale_hour = 1.0 / math.sqrt(ni * n * nj * nd)
    scale_core = 1.0 / math.sqrt(ni * n * nj * nd * kk)

    my_block = (a * rows) // tj

    def block_start(t):
        step, u = t // nb, t % nb
        target = lax.rem(b + 1 + step, nx)
        block = lax.rem(my_block + 1 + u, nb)
        return target * half + block * tj

    def count_copy(t):
        start = pl.multiple_of(block_start(t), tj)
        return pltpu.make_async_copy(counts.at[:, :, pl.ds(start, tj)], cnt.at[t], c_sem.at[t])

    for t in range(nx * nb):
        count_copy(t).start()

    barrier = pltpu.get_barrier_semaphore()
    for o in range(1, n):
        pl.semaphore_signal(barrier, inc=1, device_id={"src": lax.rem(s + o, n)}, device_id_type=MESH)
    for o in range(1, nd):
        pl.semaphore_signal(barrier, inc=1, device_id={"dst": lax.rem(d + o, nd)}, device_id_type=MESH)

    def rc(src_ref, dst_ref, send, recv, **where):
        return pltpu.make_async_remote_copy(
            src_ref=src_ref, dst_ref=dst_ref, send_sem=send, recv_sem=recv,
            device_id=where, device_id_type=MESH,
        )

    pt = 32

    def core_tile(i, carry):
        at = pl.ds(pl.multiple_of(i * pt, pt), pt)
        accs = [None] * kk
        for r in range(r3n):
            tile = core[r, at, :]
            for k in range(kk):
                term = tile * hour[k, r]
                accs[k] = term if r == 0 else accs[k] + term
        for k in range(kk):
            ch[k, at, :] = accs[k]
        return carry

    lax.fori_loop(0, r1n // pt, core_tile, 0)

    dh, dl = split(dst[...])
    d_k[...] = jnp.concatenate([dh, dh, dl], axis=1)
    d_n[...] = jnp.concatenate([dh, dl], axis=1)

    src_parts = split(src[...])
    q = src.shape[1]

    def fit_one(k, carry):
        chh, chl = split(ch[k])
        chs[k] = jnp.concatenate([chh, chh, chl], axis=1)
        pf = dot3(src_parts, (chh, chl), 1, 0)
        ph, plo = split(pf)
        pf_ks[k] = jnp.concatenate([ph, plo, ph], axis=1)
        th, tl = split(pf.T)
        pf_t[k] = jnp.concatenate([th, tl], axis=0)
        return carry

    lax.fori_loop(0, kk, fit_one, 0)
    thr[...] = jnp.zeros_like(thr)

    pl.semaphore_wait(barrier, n - 1 + nd - 1)

    r2n = dst.shape[1]
    sth, stl = split(src[...].T)

    def block_step(t, dk, dn, k, acc):
        fitted = dg(pf_ks[k], dk, 1, 1)
        m = 1.0 - cnt[t, k].astype(F32) / fitted
        mh, ml = split(m)
        wide = dg(mh, dn, 1, 0)
        thr_k = thr[k] + (wide[:, :r2n] + wide[:, r2n:] + dg(ml, dn[:, :r2n], 1, 0))
        thr[k] = thr_k
        pt_ = pf_t[k]
        tall = dg(pt_, mh, 1, 0)
        return acc + (tall[:r2n] + tall[r2n:] + dg(pt_[:r2n], ml, 1, 0)), thr_k

    def open_block(t):
        count_copy(t).wait()
        start = pl.multiple_of(block_start(t), tj)
        return start, d_k[pl.ds(start, tj), :], d_n[pl.ds(start, tj), :]

    def compute_block(t):
        start, dk, dn = open_block(t)

        def two(i, acc):
            acc, _ = block_step(t, dk, dn, 2 * i, acc)
            return block_step(t, dk, dn, 2 * i + 1, acc)[0]

        acc = lax.fori_loop(0, kk // 2, two, jnp.zeros((r2n, tj), F32))
        return acc.T, start

    q1c, q2c = [], []

    def last_block(t):
        start, dk, dn = open_block(t)
        acc = jnp.zeros((r2n, tj), F32)
        gacc = None
        for side in (1, 0):
            core_of = lax.rem(cc + side, 2)
            for oy in list(range(1, ny)) + [0]:
                peer = lax.rem(yy + oy, ny)
                first = (2 * peer + core_of) * kd
                for i in range(kd):
                    k = first + i
                    acc, thr_k = block_step(t, dk, dn, k, acc)
                    th, tl = split(thr_k)
                    wide = dg(sth, jnp.concatenate([th, tl], axis=1), 1, 0)
                    proj[k] = wide[:, :r2n] + wide[:, r2n:] + dg(stl, th, 1, 0)
                    g = dg(jnp.concatenate([th, tl, th], axis=1), chs[k], 1, 1)
                    gacc = g if gacc is None else gacc + g
                if side:
                    c = rc(proj.at[pl.ds(first, kd)], q1.at[peer], q1s.at[oy], q1r.at[oy], dst=2 * yy + core_of)
                    c.start()
                    q1c.append(c)
                else:
                    q1c[oy - 1 if oy else ny - 1].wait_recv()
                    q1[peer] = q1[peer] + proj[pl.ds(first, kd)]
                    if oy:
                        c = rc(q1.at[peer], q2.at[oy - 1], q2s.at[oy - 1], q2r.at[oy - 1], dst=2 * peer + cc)
                        c.start()
                        q2c.append(c)
        gterm[...] = gacc
        return acc.T, start

    s1, s2 = [], []
    for step in range(nx - 1):
        for u in range(nb):
            value, start = compute_block(step * nb + u)
            dacc[pl.ds(start, tj), :] = value
            slot = step * nb + u
            c = rc(dacc.at[pl.ds(start, tj), :], r1.at[slot], s1s.at[slot], s1r.at[slot],
                   src=a * nx + lax.rem(b + 1 + step, nx))
            c.start()
            s1.append(c)
    for u in range(nb):
        value, start = (last_block if u == nb - 1 else compute_block)((nx - 1) * nb + u)
        for step in range(nx - 1):
            s1[step * nb + u].wait_recv()
            value = value + r1[step * nb + u]
        dacc[pl.ds(start, tj), :] = value
        block = lax.rem(my_block + 1 + u, nb)
        last = u == nb - 1
        for i in range(cps - 1 if last else cps):
            within = lax.rem(lax.rem(a, cps) + 1 + i, cps)
            owner = block * cps + within
            o = lax.rem(owner - a + nz, nz)
            from_ = pl.ds(pl.multiple_of(start + within * rows, rows), rows)
            c = rc(dacc.at[from_, :], r2.at[o - 1], s2s.at[o - 1], s2r.at[o - 1], src=owner * nx + b)
            c.start()

    g1 = []
    for o in range(1, nd):
        peer = lax.rem(d + o, nd)
        c = rc(gterm.at[pl.ds(pl.multiple_of(peer * irows, irows), irows), :], r3.at[o - 1], gs1s.at[o - 1], gs1r.at[o - 1],
               dst=peer)
        c.start()
        g1.append(c)

    ysum = q1[yy]
    for o in range(1, ny):
        q2c[o - 1].wait_recv()
        ysum = ysum + q2[o - 1]
    for i in range(n):
        pq[i] = ysum[:, i * share:(i + 1) * share, :]
    q3c = []
    for o in range(1, n):
        peer = lax.rem(s + o, n)
        c = rc(pq.at[peer], q3.at[o - 1], q3s.at[o - 1], q3r.at[o - 1], src=peer)
        c.start()
        q3c.append(c)

    mine = pl.ds(pl.multiple_of((b * nz + a) * rows, rows), rows)
    total = dacc[mine, :]
    z_wait = []
    for o in range(1, nz):
        c = rc(dacc.at[mine, :], r2.at[o - 1], s2s.at[o - 1], s2r.at[o - 1], src=lax.rem(a + o, nz) * nx + b)
        c.wait_recv()
        z_wait.append(c)
        total = total + r2[o - 1]
    g_dst[mine, :] = total * scale_dst

    def x_copy(step, o):
        at = pl.ds(pl.multiple_of((b * nz + lax.rem(a - o + nz, nz)) * rows, rows), rows)
        slot = step * nz + o
        return rc(g_dst.at[at, :], g_dst.at[at, :], xs.at[slot], xr.at[slot],
                  src=a * nx + lax.rem(b + 1 + step, nx))

    zc = []
    for o in range(1, nz):
        c = rc(g_dst.at[mine, :], g_dst.at[mine, :], zs.at[o - 1], zr.at[o - 1],
               src=lax.rem(a + o, nz) * nx + b)
        c.start()
        zc.append(c)
    xc = []
    for step in range(nx - 1):
        c = x_copy(step, 0)
        c.start()
        xc.append(c)

    def hour_row(r, carry):
        for k in range(kk):
            acc = core[r, 0:8, :] * proj[k, 0:8, :]
            for i in range(1, r1n // 8):
                acc = acc + core[r, 8 * i:8 * i + 8, :] * proj[k, 8 * i:8 * i + 8, :]
            hacc[k, r] = acc
        return carry

    lax.fori_loop(0, r3n, hour_row, 0)
    hl = jnp.sum(jnp.sum(hacc[...], axis=2), axis=2)
    hl = jnp.concatenate([hl, jnp.zeros((kk, hd.shape[2] - r3n), F32)], axis=1)
    hd[d] = hl
    h1 = []
    for o in range(1, nd):
        c = rc(hd.at[d], hd.at[d], hds.at[o - 1], hdr.at[o - 1], dst=lax.rem(d + o, nd))
        c.start()
        h1.append(c)

    own_rows = pl.ds(pl.multiple_of(d * irows, irows), irows)
    gsum = gterm[own_rows, :]
    for o in range(1, nd):
        g1[o - 1].wait_recv()
        gsum = gsum + r3[o - 1]
    g_src[own_rows, :] = gsum * scale_src
    g2 = []
    for o in range(1, nd):
        c = rc(g_src.at[own_rows, :], g_src.at[own_rows, :], gs2s.at[o - 1], gs2r.at[o - 1], dst=lax.rem(d + o, nd))
        c.start()
        g2.append(c)

    psum = pq[s]
    for o in range(1, n):
        q3c[o - 1].wait_recv()
        psum = psum + q3[o - 1]
    pk[d] = psum
    pkc = []
    for o in range(1, nd):
        c = rc(pk.at[d], pk.at[d], pks.at[o - 1], pkr.at[o - 1], dst=lax.rem(d + o, nd))
        c.start()
        pkc.append(c)

    for o in range(1, nd):
        h1[o - 1].wait_recv()
    hsum = hd[0]
    for i in range(1, nd):
        hsum = hsum + hd[i]
    hs[s] = hsum
    h2 = []
    for o in range(1, n):
        c = rc(hs.at[s], hs.at[s], hss.at[o - 1], hsr.at[o - 1], src=lax.rem(s + o, n))
        c.start()
        h2.append(c)

    for o in range(1, nz):
        zc[o - 1].wait_recv()
        for step in range(nx - 1):
            c = x_copy(step, o)
            c.start()
            xc.append(c)

    for o in range(1, n):
        h2[o - 1].wait_recv()
    htot = hs[0]
    for i in range(1, n):
        htot = htot + hs[i]
    g_hour[...] = htot[:, :r3n] * scale_hour

    for o in range(1, nd):
        pkc[o - 1].wait_recv()
    tiles = [pk[k // kd, k % kd] * scale_core for k in range(kk)]
    for r in range(r3n):
        acc = tiles[0] * hour[0, r]
        for k in range(1, kk):
            acc = acc + tiles[k] * hour[k, r]
        g_core[r] = acc

    for c in g2:
        c.wait_recv()
    for c in xc:
        c.wait_recv()
    for c in s1 + z_wait + zc + xc + g1 + g2 + q1c + q2c + q3c + pkc + h1 + h2:
        c.wait_send()


def write_out(*refs):
    half = len(refs) // 3
    ins, outs, sems = refs[:half], refs[half:2 * half], refs[2 * half:]
    copies = [pltpu.make_async_copy(i, o, m) for i, o, m in zip(ins, outs, sems)]
    for c in copies:
        c.start()
    for c in copies:
        c.wait()


def solution(mesh):
    n = mesh.shape["src"]
    nd = mesh.shape["dst"]
    nx = 2 ** (int(math.log2(n)) // 2)
    nz = n // nx
    ny = nd // 2

    def shards(counts, src, dst, hour, core):
        kk, ni, nj = counts.shape
        r3n, r1n, r2n = core.shape
        rows = nj // n
        half = nj // nx
        tj = min(256, half)
        nb = half // tj
        kd = kk // nd
        share = r1n // n
        irows = ni // nd
        vm = pl.BlockSpec(memory_space=pltpu.VMEM)
        dma = lambda *shape: pltpu.SemaphoreType.DMA(shape)
        f = lambda *shape: pltpu.VMEM(shape, F32)
        h = lambda *shape: pltpu.VMEM(shape, BF16)
        pair = lambda m: [dma(m), dma(m)]
        scratch = [
            pltpu.VMEM((nx * nb, kk, ni, tj), jnp.int32),
            f(kk, r1n, r2n), h(kk, ni, 3 * r2n), h(kk, 2 * r2n, ni), h(nj, 3 * r2n), h(nj, 2 * r2n),
            f(kk, ni, r2n), f(nj, r2n), f((nx - 1) * nb, tj, r2n), f(nz - 1, rows, r2n),
            h(kk, r1n, 3 * r2n), f(ni, r1n), f(nd - 1, irows, r1n), f(kk, r1n, r2n), f(ny, kd, r1n, r2n), f(ny - 1, kd, r1n, r2n),
            f(n, kd, share, r2n), f(n - 1, kd, share, r2n), f(nd, kd, share, r2n), f(kk, r3n, 8, r2n),
            f(nd, kk, 128), f(n, kk, 128),
            dma(nx * nb),
        ]
        for m in ((nx - 1) * nb, nz - 1, nz - 1, (nx - 1) * nz, nd - 1, nd - 1, ny, ny - 1, n - 1, nd - 1, nd - 1, n - 1):
            scratch += pair(m)
        shapes = ((ni, r1n), (nj, r2n), (kk, r3n), (r3n, share, r2n))
        results = pl.pallas_call(
            functools.partial(kernel, n, nz, nx, nd, tj),
            out_shape=tuple(pltpu.VMEM(x, F32) for x in shapes),
            in_specs=[pl.BlockSpec(memory_space=pl.ANY), vm, vm, pl.BlockSpec(memory_space=pltpu.SMEM), vm],
            out_specs=(vm, vm, vm, vm),
            scratch_shapes=scratch,
            compiler_params=pltpu.CompilerParams(
                collective_id=0, has_side_effects=True, vmem_limit_bytes=60 * 1024 * 1024
            ),
        )(counts, src, dst, hour, core)
        return pl.pallas_call(
            write_out,
            out_shape=tuple(jax.ShapeDtypeStruct(x, F32) for x in shapes),
            in_specs=[vm] * 4,
            out_specs=(pl.BlockSpec(memory_space=pl.ANY),) * 4,
            scratch_shapes=[pltpu.SemaphoreType.DMA] * 4,
        )(*(pltpu.with_memory_space_constraint(x, pltpu.VMEM) for x in results))

    in_specs = (P(None, "src", "dst"), P("src", None), P("dst", None), P(), P())
    out_specs = (P("src", None), P("dst", None), P(), P(None, "src", None))
    return jax.shard_map(shards, mesh=mesh, in_specs=in_specs, out_specs=out_specs, check_vma=False)
```

profile of v0, /device:TPU:0, one launch (start us, length us, event | category | flops | bytes accessed | tf_op | source)
XLA Modules:
  0.0 43.5 jit_solution(12795039704686179724)
XLA Ops:
  0.6 41.9 %shard_map.84 = (f32[256,128]{1,0:T(8,128)S(1)}, f32[1024,128]{1,0:T(8,128)S(1)}, f32[8,32]{1,0:T(8,128)S(1)}, f32[32,16,128]{2,1,0:T(8,128)S(1)}) custom-call(s32[8,256,1024]{2,1,0:T(8,128)} %counts.1, f32[256,128]{1,0:T(8,128)} %src.1, f32[1024,128]{1,0:T(8,128)} %dst.1, f32[8,32]{1,0:T(8,128)} %hour.1, f32[32,128,128]{2,1,0:T(8,128)} %core.1), custom_call_target="tpu_custom_call" | custom-call | tf_op jit(solution)/shard_map/pallas_call | solution.py:394
  42.6 1.0 %shard_map.85 = (f32[256,128]{1,0:T(8,128)}, f32[1024,128]{1,0:T(8,128)}, f32[8,32]{1,0:T(8,128)}, f32[32,16,128]{2,1,0:T(8,128)}) custom-call(f32[256,128]{1,0:T(8,128)S(1)} %get-tuple-element.8.refs_0_, f32[1024,128]{1,0:T(8,128)S(1)} %get-tuple-element.9.refs_1_, f32[8,32]{1,0:T(8,128)S(1)} %get-tuple-element.10.refs_2_, ...), custom_call_target="tpu_custom_call" | custom-call | tf_op jit(solution)/shard_map/pallas_call | solution.py:404
where the time goes:
time: 43.7 us; the launch traced here: 43.5 us
  Pallas kernels  42.9 us (98%)
  between operations  0.64 us (1%)
    pallas_call x1, Pallas kernels, shards(): pl.pallas_call(functools.partial(kernel, n, nz, nx, nd, tj), out_shape=tu...  41.9 us
    pallas_call x1, Pallas kernels, shards(): pl.pallas_call(write_out, out_shape=tuple((jax.ShapeDtypeStruct(x, F32) f...  0.96 us

commit v1 on v0

v1 whole, which is shorter than its diff:
```python
import functools
import math

import jax
import jax.numpy as jnp
from jax import lax
from jax.experimental import pallas as pl
from jax.experimental.pallas import tpu as pltpu
from jax.sharding import PartitionSpec as P

F32 = jnp.float32
BF16 = jnp.bfloat16
MESH = pl.DeviceIdType.MESH


def split(x):
    hi = x.astype(BF16)
    lo = (x - hi.astype(F32)).astype(BF16)
    return hi, lo


def dg(a, b, ca, cb):
    return lax.dot_general(a, b, (((ca,), (cb,)), ((), ())), preferred_element_type=F32)


def dot3(a, b, ca, cb):
    ah, al = a
    bh, bl = b
    return dg(ah, bh, ca, cb) + dg(ah, bl, ca, cb) + dg(al, bh, ca, cb)


def kernel(
    n, nz, nx, nd, nh, tj,
    counts, src_in, dst_in, hour, core_in,
    g_src, g_dst, g_hour, g_core,
    src, dst, core, cnt, ch, pf_ks, pf_t, d_k, d_n, thr, dacc, r1, r2,
    chs, gterm, r3, proj, q1, q2, pq, q3, pk, hacc, hd, hs, msc, accr,
    i_sem, c_sem, s1s, s1r, s2s, s2r, zs, zr, xs, xr,
    gs1s, gs1r, gs2s, gs2r, q1s, q1r, q2s, q2r, q3s, q3r, pks, pkr, hds, hdr, hss, hsr,
):
    s = lax.axis_index("src")
    d = lax.axis_index("dst")
    a = s // nx
    b = lax.rem(s, nx)
    yy = d // 2
    cc = lax.rem(d, 2)
    ny = nd // 2
    kk, ni, _ = counts.shape
    nj = dst.shape[0]
    r3n = core.shape[0]
    r1n = core.shape[1]
    r2n = dst.shape[1]
    half = nj // nx
    zrows = tj // nz
    kd = kk // nd
    share = r1n // n
    irows = ni // nd
    nt = nh * nx
    scale_src = 1.0 / math.sqrt(nj * nd * kk)
    scale_dst = 1.0 / math.sqrt(ni * n * kk)
    scale_hour = 1.0 / math.sqrt(ni * n * nj * nd)
    scale_core = 1.0 / math.sqrt(ni * n * nj * nd * kk)

    dst_copy = pltpu.make_async_copy(dst_in, dst, i_sem.at[0])
    core_copy = pltpu.make_async_copy(core_in, core, i_sem.at[1])
    src_copy = pltpu.make_async_copy(src_in, src, i_sem.at[2])
    for c in (dst_copy, core_copy, src_copy):
        c.start()

    def block_start(t):
        return lax.rem(b + 1 + t % nx, nx) * half + (t // nx) * tj

    def count_copy(t):
        start = pl.multiple_of(block_start(t), tj)
        return pltpu.make_async_copy(counts.at[:, :, pl.ds(start, tj)], cnt.at[t], c_sem.at[t])

    for t in range(nt):
        count_copy(t).start()

    barrier = pltpu.get_barrier_semaphore()
    for o in range(1, n):
        pl.semaphore_signal(barrier, inc=1, device_id={"src": lax.rem(s + o, n)}, device_id_type=MESH)
    for o in range(1, nd):
        pl.semaphore_signal(barrier, inc=1, device_id={"dst": lax.rem(d + o, nd)}, device_id_type=MESH)

    def rc(src_ref, dst_ref, send, recv, **where):
        return pltpu.make_async_remote_copy(
            src_ref=src_ref, dst_ref=dst_ref, send_sem=send, recv_sem=recv,
            device_id=where, device_id_type=MESH,
        )

    dst_copy.wait()
    dh, dl = split(dst[...])
    d_n[...] = jnp.concatenate([dh, dl], axis=1)
    dth, dtl = split(dst[...].T)
    d_k[...] = jnp.concatenate([dth, dth, dtl], axis=0)
    thr[...] = jnp.zeros_like(thr)
    accr[...] = jnp.zeros_like(accr)

    core_copy.wait()
    pt = 32

    def core_tile(i, carry):
        at = pl.ds(pl.multiple_of(i * pt, pt), pt)
        accs = [None] * kk
        for r in range(r3n):
            tile = core[r, at, :]
            for k in range(kk):
                term = tile * hour[k, r]
                accs[k] = term if r == 0 else accs[k] + term
        for k in range(kk):
            ch[k, at, :] = accs[k]
        return carry

    lax.fori_loop(0, r1n // pt, core_tile, 0)

    src_copy.wait()
    src_parts = split(src[...])

    def fit_one(k, carry):
        chh, chl = split(ch[k])
        chs[k] = jnp.concatenate([chh, chh, chl], axis=1)
        pf = dot3(src_parts, (chh, chl), 1, 0)
        ph, plo = split(pf)
        pf_ks[k] = jnp.concatenate([ph, plo, ph], axis=1)
        th, tl = split(pf.T)
        pf_t[k] = jnp.concatenate([th, tl], axis=0)
        return carry

    lax.fori_loop(0, kk, fit_one, 0)
    sth, stl = split(src[...].T)

    def misfit(t, start, k, slot):
        at = pl.ds(pl.multiple_of(start, tj), tj)
        fitted = dg(pf_ks[pl.ds(k, kd)].reshape(kd * ni, 3 * r2n), d_k[:, at], 1, 0)
        m = 1.0 - cnt[t, pl.ds(k, kd)].reshape(kd * ni, tj).astype(F32) / fitted
        mh, ml = split(m)
        msc[slot, 0] = mh
        msc[slot, 1] = ml

    def gather_terms(start, k, slot):
        dn = d_n[pl.ds(pl.multiple_of(start, tj), tj), :]
        mh = msc[slot, 0]
        ml = msc[slot, 1]
        wide = dg(mh, dn, 1, 0)
        new = thr[pl.ds(k, kd)].reshape(kd * ni, r2n) + (wide[:, :r2n] + wide[:, r2n:] + dg(ml, dn[:, :r2n], 1, 0))
        thr[pl.ds(k, kd)] = new.reshape(kd, ni, r2n)
        acc = accr[...]
        for e in range(kd):
            pt_ = pf_t[k + e]
            rows = slice(e * ni, (e + 1) * ni)
            tall = dg(pt_, mh[rows], 1, 0)
            acc = acc + (tall[:r2n] + tall[r2n:] + dg(pt_[:r2n], ml[rows], 1, 0))
        accr[...] = acc
        return new

    groups = [(side, oy) for side in (1, 0) for oy in list(range(1, ny)) + [0]]

    def group_first(g):
        side, oy = groups[g]
        return (2 * lax.rem(yy + oy, ny) + lax.rem(cc + side, 2)) * kd

    first_hour = group_first(0)
    pairs = kk // (2 * kd)

    def compute_block(t):
        count_copy(t + 1).wait()
        start = block_start(t)
        after = block_start(t + 1)
        after_k = first_hour if t + 1 == nt - 1 else 0

        def two(i, carry):
            k = 2 * kd * i
            misfit(t, start, k + kd, 1)
            gather_terms(start, k, 0)
            end = (i + 1) // pairs
            misfit(t + end, start + end * (after - start), (1 - end) * (k + 2 * kd) + end * after_k, 0)
            gather_terms(start, k + kd, 1)
            return carry

        lax.fori_loop(0, pairs, two, 0)
        dacc[pl.ds(pl.multiple_of(start, tj), tj), :] = accr[...].T
        accr[...] = jnp.zeros_like(accr)

    s1, s2, zc, xc = [], [], {}, []

    def x_send(t):
        h, step = t // nx, t % nx
        at = pl.ds(pl.multiple_of(block_start(t), tj), tj)
        slot = h * (nx - 1) + step
        c = rc(dacc.at[at, :], r1.at[slot], s1s.at[slot], s1r.at[slot], src=a * nx + lax.rem(b + 1 + step, nx))
        c.start()
        s1.append(c)

    def z_piece(h, owner):
        return pl.ds(pl.multiple_of(b * half + h * tj + owner * zrows, zrows), zrows)

    def z_send(h):
        own = pl.ds(pl.multiple_of(b * half + h * tj, tj), tj)
        value = dacc[own, :]
        for step in range(nx - 1):
            s1[h * (nx - 1) + step].wait_recv()
            value = value + r1[h * (nx - 1) + step]
        dacc[own, :] = value
        for o in range(1, nz):
            owner = lax.rem(a + o, nz)
            slot = h * (nz - 1) + o - 1
            c = rc(dacc.at[z_piece(h, owner), :], r2.at[slot], s2s.at[slot], s2r.at[slot], src=owner * nx + b)
            c.start()
            s2.append(c)

    def x_copy(h, step, o):
        at = z_piece(h, lax.rem(a - o + nz, nz))
        slot = (h * (nx - 1) + step) * nz + o
        return rc(g_dst.at[at, :], g_dst.at[at, :], xs.at[slot], xr.at[slot],
                  src=a * nx + lax.rem(b + 1 + step, nx))

    def x_forward(h, o):
        for step in range(nx - 1):
            c = x_copy(h, step, o)
            c.start()
            xc.append(c)

    def finish(h):
        mine = z_piece(h, a)
        total = dacc[mine, :]
        for o in range(1, nz):
            s2[h * (nz - 1) + o - 1].wait_recv()
            total = total + r2[h * (nz - 1) + o - 1]
        g_dst[mine, :] = total * scale_dst
        x_forward(h, 0)
        for o in range(1, nz):
            slot = h * (nz - 1) + o - 1
            c = rc(g_dst.at[mine, :], g_dst.at[mine, :], zs.at[slot], zr.at[slot], src=lax.rem(a + o, nz) * nx + b)
            c.start()
            zc[h, o] = c

    def forward(h):
        for o in range(1, nz):
            zc[h, o].wait_recv()
            x_forward(h, o)

    q1c, q2c = [], []

    def last_block(t):
        start = block_start(t)
        gacc = None
        for g, (side, oy) in enumerate(groups):
            slot = g % 2
            first = group_first(g)
            if g + 1 < nd:
                misfit(t, start, group_first(g + 1), 1 - slot)
            new = gather_terms(start, first, slot)
            th, tl = split(new)
            for e in range(kd):
                rows = slice(e * ni, (e + 1) * ni)
                wide = dg(sth, jnp.concatenate([th[rows], tl[rows]], axis=1), 1, 0)
                proj[first + e] = wide[:, :r2n] + wide[:, r2n:] + dg(stl, th[rows], 1, 0)
                term = dg(jnp.concatenate([th[rows], tl[rows], th[rows]], axis=1), chs[first + e], 1, 1)
                gacc = term if gacc is None else gacc + term
            core_of = lax.rem(cc + side, 2)
            peer = lax.rem(yy + oy, ny)
            if side:
                c = rc(proj.at[pl.ds(first, kd)], q1.at[peer], q1s.at[oy], q1r.at[oy], dst=2 * yy + core_of)
                c.start()
                q1c.append(c)
            else:
                q1c[oy - 1 if oy else ny - 1].wait_recv()
                q1[peer] = q1[peer] + proj[pl.ds(first, kd)]
                if oy:
                    c = rc(q1.at[peer], q2.at[oy - 1], q2s.at[oy - 1], q2r.at[oy - 1], dst=2 * peer + cc)
                    c.start()
                    q2c.append(c)
            if g == nd // 2 - 1:
                for h in range(nh - 1):
                    z_send(h)
        gterm[...] = gacc
        dacc[pl.ds(pl.multiple_of(start, tj), tj), :] = accr[...].T

    count_copy(0).wait()
    misfit(0, block_start(0), 0 if nt > 1 else first_hour, 0)
    for t in range(nt - 1):
        compute_block(t)
        if t == 0:
            pl.semaphore_wait(barrier, n - 1 + nd - 1)
        if t % nx < nx - 1:
            x_send(t)
    last_block(nt - 1)

    g1 = []
    for o in range(1, nd):
        peer = lax.rem(d + o, nd)
        c = rc(gterm.at[pl.ds(pl.multiple_of(peer * irows, irows), irows), :], r3.at[o - 1], gs1s.at[o - 1], gs1r.at[o - 1],
               dst=peer)
        c.start()
        g1.append(c)

    z_send(nh - 1)

    ysum = q1[yy]
    for o in range(1, ny):
        q2c[o - 1].wait_recv()
        ysum = ysum + q2[o - 1]
    for i in range(n):
        pq[i] = ysum[:, i * share:(i + 1) * share, :]
    q3c = []
    for o in range(1, n):
        peer = lax.rem(s + o, n)
        c = rc(pq.at[peer], q3.at[o - 1], q3s.at[o - 1], q3r.at[o - 1], src=peer)
        c.start()
        q3c.append(c)

    for h in range(nh - 1):
        finish(h)

    def hour_row(r, carry):
        for k in range(kk):
            acc = core[r, 0:8, :] * proj[k, 0:8, :]
            for i in range(1, r1n // 8):
                acc = acc + core[r, 8 * i:8 * i + 8, :] * proj[k, 8 * i:8 * i + 8, :]
            hacc[k, r] = acc
        return carry

    lax.fori_loop(0, r3n, hour_row, 0)
    hl = jnp.sum(jnp.sum(hacc[...], axis=2), axis=2)
    hl = jnp.concatenate([hl, jnp.zeros((kk, hd.shape[2] - r3n), F32)], axis=1)
    hd[d] = hl
    h1 = []
    for o in range(1, nd):
        c = rc(hd.at[d], hd.at[d], hds.at[o - 1], hdr.at[o - 1], dst=lax.rem(d + o, nd))
        c.start()
        h1.append(c)

    own_rows = pl.ds(pl.multiple_of(d * irows, irows), irows)
    gsum = gterm[own_rows, :]
    for o in range(1, nd):
        g1[o - 1].wait_recv()
        gsum = gsum + r3[o - 1]
    g_src[own_rows, :] = gsum * scale_src
    g2 = []
    for o in range(1, nd):
        c = rc(g_src.at[own_rows, :], g_src.at[own_rows, :], gs2s.at[o - 1], gs2r.at[o - 1], dst=lax.rem(d + o, nd))
        c.start()
        g2.append(c)

    finish(nh - 1)

    for o in range(1, nd):
        h1[o - 1].wait_recv()
    hsum = hd[0]
    for i in range(1, nd):
        hsum = hsum + hd[i]
    hs[s] = hsum
    h2 = []
    for o in range(1, n):
        c = rc(hs.at[s], hs.at[s], hss.at[o - 1], hsr.at[o - 1], src=lax.rem(s + o, n))
        c.start()
        h2.append(c)

    psum = pq[s]
    for o in range(1, n):
        q3c[o - 1].wait_recv()
        psum = psum + q3[o - 1]
    pk[d] = psum
    pkc = []
    for o in range(1, nd):
        c = rc(pk.at[d], pk.at[d], pks.at[o - 1], pkr.at[o - 1], dst=lax.rem(d + o, nd))
        c.start()
        pkc.append(c)

    for h in range(nh):
        forward(h)

    for o in range(1, n):
        h2[o - 1].wait_recv()
    htot = hs[0]
    for i in range(1, n):
        htot = htot + hs[i]
    g_hour[...] = htot[:, :r3n] * scale_hour

    for o in range(1, nd):
        pkc[o - 1].wait_recv()
    tiles = [pk[k // kd, k % kd] * scale_core for k in range(kk)]
    for r in range(r3n):
        acc = tiles[0] * hour[0, r]
        for k in range(1, kk):
            acc = acc + tiles[k] * hour[k, r]
        g_core[r] = acc

    for c in g2:
        c.wait_recv()
    for c in xc:
        c.wait_recv()
    for c in s1 + s2 + list(zc.values()) + xc + g1 + g2 + q1c + q2c + q3c + pkc + h1 + h2:
        c.wait_send()


def write_out(*refs):
    half = len(refs) // 3
    ins, outs, sems = refs[:half], refs[half:2 * half], refs[2 * half:]
    copies = [pltpu.make_async_copy(i, o, m) for i, o, m in zip(ins, outs, sems)]
    for c in copies:
        c.start()
    for c in copies:
        c.wait()


def solution(mesh):
    n = mesh.shape["src"]
    nd = mesh.shape["dst"]
    nx = 2 ** (int(math.log2(n)) // 2)
    nz = n // nx
    ny = nd // 2

    def shards(counts, src, dst, hour, core):
        kk, ni, nj = counts.shape
        r3n, r1n, r2n = core.shape
        tj = min(256, nj // nx)
        nh = nj // (nx * tj)
        kd = kk // nd
        share = r1n // n
        irows = ni // nd
        vm = pl.BlockSpec(memory_space=pltpu.VMEM)
        hbm = pl.BlockSpec(memory_space=pl.ANY)
        dma = lambda *shape: pltpu.SemaphoreType.DMA(shape)
        f = lambda *shape: pltpu.VMEM(shape, F32)
        h = lambda *shape: pltpu.VMEM(shape, BF16)
        pair = lambda m: [dma(m), dma(m)]
        scratch = [
            f(ni, r1n), f(nj, r2n), f(r3n, r1n, r2n), pltpu.VMEM((nh * nx, kk, ni, tj), jnp.int32),
            f(kk, r1n, r2n), h(kk, ni, 3 * r2n), h(kk, 2 * r2n, ni), h(3 * r2n, nj), h(nj, 2 * r2n),
            f(kk, ni, r2n), f(nj, r2n), f(nh * (nx - 1), tj, r2n), f(nh * (nz - 1), tj // nz, r2n),
            h(kk, r1n, 3 * r2n), f(ni, r1n), f(nd - 1, irows, r1n), f(kk, r1n, r2n), f(ny, kd, r1n, r2n), f(ny - 1, kd, r1n, r2n),
            f(n, kd, share, r2n), f(n - 1, kd, share, r2n), f(nd, kd, share, r2n), f(kk, r3n, 8, r2n),
            f(nd, kk, 128), f(n, kk, 128), h(2, 2, kd * ni, tj), f(r2n, tj),
            dma(3), dma(nh * nx),
        ]
        for m in (nh * (nx - 1), nh * (nz - 1), nh * (nz - 1), nh * (nx - 1) * nz, nd - 1, nd - 1, ny, ny - 1, n - 1, nd - 1, nd - 1, n - 1):
            scratch += pair(m)
        shapes = ((ni, r1n), (nj, r2n), (kk, r3n), (r3n, share, r2n))
        results = pl.pallas_call(
            functools.partial(kernel, n, nz, nx, nd, nh, tj),
            out_shape=tuple(pltpu.VMEM(x, F32) for x in shapes),
            in_specs=[hbm, hbm, hbm, pl.BlockSpec(memory_space=pltpu.SMEM), hbm],
            out_specs=(vm, vm, vm, vm),
            scratch_shapes=scratch,
            compiler_params=pltpu.CompilerParams(
                collective_id=0, has_side_effects=True, vmem_limit_bytes=60 * 1024 * 1024
            ),
        )(counts, src, dst, hour, core)
        return pl.pallas_call(
            write_out,
            out_shape=tuple(jax.ShapeDtypeStruct(x, F32) for x in shapes),
            in_specs=[vm] * 4,
            out_specs=(pl.BlockSpec(memory_space=pl.ANY),) * 4,
            scratch_shapes=[pltpu.SemaphoreType.DMA] * 4,
        )(*(pltpu.with_memory_space_constraint(x, pltpu.VMEM) for x in results))

    in_specs = (P(None, "src", "dst"), P("src", None), P("dst", None), P(), P())
    out_specs = (P("src", None), P("dst", None), P(), P(None, "src", None))
    return jax.shard_map(shards, mesh=mesh, in_specs=in_specs, out_specs=out_specs, check_vma=False)
```

time: 43.7 us -> 40.9 us (0.936)
  Pallas kernels: 42.9 us -> 40 us
    pallas_call x1, Pallas kernels: 41.9 us -> 39.1 us  [shards(): pl.pallas_call(functools.partial(kernel, n, nz, nx, nd, nh, tj), out_shap...]
where the time goes in v1:
time: 40.9 us; the launch traced here: 40.7 us
  Pallas kernels  40 us (98%)
  between operations  0.64 us (2%)
    pallas_call x1, Pallas kernels, shards(): pl.pallas_call(functools.partial(kernel, n, nz, nx, nd, nh, tj), out_shap...  39.1 us
    pallas_call x1, Pallas kernels, shards(): pl.pallas_call(write_out, out_shape=tuple((jax.ShapeDtypeStruct(x, F32) f...  0.96 us

profile of v1, /device:TPU:0, one launch (start us, length us, event | category | flops | bytes accessed | tf_op | source)
XLA Modules:
  0.0 40.7 jit_solution(13579907326991324063)
XLA Ops:
  0.6 39.1 %shard_map.84 = (f32[256,128]{1,0:T(8,128)S(1)}, f32[1024,128]{1,0:T(8,128)S(1)}, f32[8,32]{1,0:T(8,128)S(1)}, f32[32,16,128]{2,1,0:T(8,128)S(1)}) custom-call(s32[8,256,1024]{2,1,0:T(8,128)} %counts.1, f32[256,128]{1,0:T(8,128)} %src_in.1, f32[1024,128]{1,0:T(8,128)} %dst_in.1, f32[8,32]{1,0:T(8,128)} %hour.1, f32[32,128,128]{2,1,0:T(8,128)} %core_in.1), custom_call_target="tpu_custom_call" | custom-call | tf_op jit(solution)/shard_map/pallas_call | solution.py:441
  39.7 1.0 %shard_map.85 = (f32[256,128]{1,0:T(8,128)}, f32[1024,128]{1,0:T(8,128)}, f32[8,32]{1,0:T(8,128)}, f32[32,16,128]{2,1,0:T(8,128)}) custom-call(f32[256,128]{1,0:T(8,128)S(1)} %get-tuple-element.8.refs_0_, f32[1024,128]{1,0:T(8,128)S(1)} %get-tuple-element.9.refs_1_, f32[8,32]{1,0:T(8,128)S(1)} %get-tuple-element.10.refs_2_, ...), custom_call_target="tpu_custom_call" | custom-call | tf_op jit(solution)/shard_map/pallas_call | solution.py:451

commit v2 on v1

--- a/solution.py
+++ b/solution.py
@@ -34,7 +34,7 @@
     counts, src_in, dst_in, hour, core_in,
     g_src, g_dst, g_hour, g_core,
     src, dst, core, cnt, ch, pf_ks, pf_t, d_k, d_n, thr, dacc, r1, r2,
-    chs, gterm, r3, proj, q1, q2, pq, q3, pk, hacc, hd, hs, msc, accr,
+    chs, gterm, r3, proj, q1, q2, pq, q3, pk, hacc, hd, hs, msc,
     i_sem, c_sem, s1s, s1r, s2s, s2r, zs, zr, xs, xr,
     gs1s, gs1r, gs2s, gs2r, q1s, q1r, q2s, q2r, q3s, q3r, pks, pkr, hds, hdr, hss, hsr,
 ):
@@ -68,7 +68,16 @@
         c.start()
 
     def block_start(t):
-        return lax.rem(b + 1 + t % nx, nx) * half + (t // nx) * tj
+        return lax.rem(b + 1 + t // nh, nx) * half + (t % nh) * tj
+
+    def flip(e):
+        out = a
+        for bit in range(e.bit_length()):
+            if (e >> bit) % 2:
+                out = out + (1 << bit) * (1 - 2 * lax.rem(a // (1 << bit), 2))
+        return out
+
+    far_first = list(range(nz - 1, 0, -1))
 
     def count_copy(t):
         start = pl.multiple_of(block_start(t), tj)
@@ -94,8 +103,6 @@
     d_n[...] = jnp.concatenate([dh, dl], axis=1)
     dth, dtl = split(dst[...].T)
     d_k[...] = jnp.concatenate([dth, dth, dtl], axis=0)
-    thr[...] = jnp.zeros_like(thr)
-    accr[...] = jnp.zeros_like(accr)
 
     core_copy.wait()
     pt = 32
@@ -130,87 +137,83 @@
     lax.fori_loop(0, kk, fit_one, 0)
     sth, stl = split(src[...].T)
 
-    def misfit(t, start, k, slot):
-        at = pl.ds(pl.multiple_of(start, tj), tj)
-        fitted = dg(pf_ks[pl.ds(k, kd)].reshape(kd * ni, 3 * r2n), d_k[:, at], 1, 0)
-        m = 1.0 - cnt[t, pl.ds(k, kd)].reshape(kd * ni, tj).astype(F32) / fitted
+    def misfit(t, g):
+        at = pl.ds(pl.multiple_of(block_start(t), tj), tj)
+        hours = slice(g * kd, (g + 1) * kd)
+        fitted = dg(pf_ks[hours].reshape(kd * ni, 3 * r2n), d_k[:, at], 1, 0)
+        m = 1.0 - cnt[t, hours].reshape(kd * ni, tj).astype(F32) / fitted
         mh, ml = split(m)
-        msc[slot, 0] = mh
-        msc[slot, 1] = ml
-
-    def gather_terms(start, k, slot):
-        dn = d_n[pl.ds(pl.multiple_of(start, tj), tj), :]
-        mh = msc[slot, 0]
-        ml = msc[slot, 1]
-        wide = dg(mh, dn, 1, 0)
-        new = thr[pl.ds(k, kd)].reshape(kd * ni, r2n) + (wide[:, :r2n] + wide[:, r2n:] + dg(ml, dn[:, :r2n], 1, 0))
-        thr[pl.ds(k, kd)] = new.reshape(kd, ni, r2n)
-        acc = accr[...]
+        msc[t, g, 0] = mh
+        msc[t, g, 1] = ml
+
+    def add_tall(t, g, acc):
         for e in range(kd):
-            pt_ = pf_t[k + e]
+            pt_ = pf_t[g * kd + e]
             rows = slice(e * ni, (e + 1) * ni)
-            tall = dg(pt_, mh[rows], 1, 0)
-            acc = acc + (tall[:r2n] + tall[r2n:] + dg(pt_[:r2n], ml[rows], 1, 0))
-        accr[...] = acc
-        return new
+            tall = dg(pt_, msc[t, g, 0, rows], 1, 0)
+            new = tall[:r2n] + tall[r2n:] + dg(pt_[:r2n], msc[t, g, 1, rows], 1, 0)
+            acc = new if acc is None else acc + new
+        return acc
+
+    def through(gi):
+        out = None
+        for t in range(nt):
+            dn = d_n[pl.ds(pl.multiple_of(block_start(t), tj), tj), :]
+            wide = dg(msc[t, gi, 0], dn, 1, 0)
+            new = wide[:, :r2n] + wide[:, r2n:] + dg(msc[t, gi, 1], dn[:, :r2n], 1, 0)
+            out = new if out is None else out + new
+        return out
 
     groups = [(side, oy) for side in (1, 0) for oy in list(range(1, ny)) + [0]]
 
-    def group_first(g):
+    def group_of(g):
         side, oy = groups[g]
-        return (2 * lax.rem(yy + oy, ny) + lax.rem(cc + side, 2)) * kd
-
-    first_hour = group_first(0)
-    pairs = kk // (2 * kd)
+        return 2 * lax.rem(yy + oy, ny) + lax.rem(cc + side, 2)
 
     def compute_block(t):
-        count_copy(t + 1).wait()
-        start = block_start(t)
-        after = block_start(t + 1)
-        after_k = first_hour if t + 1 == nt - 1 else 0
-
-        def two(i, carry):
-            k = 2 * kd * i
-            misfit(t, start, k + kd, 1)
-            gather_terms(start, k, 0)
-            end = (i + 1) // pairs
-            misfit(t + end, start + end * (after - start), (1 - end) * (k + 2 * kd) + end * after_k, 0)
-            gather_terms(start, k + kd, 1)
-            return carry
-
-        lax.fori_loop(0, pairs, two, 0)
-        dacc[pl.ds(pl.multiple_of(start, tj), tj), :] = accr[...].T
-        accr[...] = jnp.zeros_like(accr)
-
-    s1, s2, zc, xc = [], [], {}, []
-
-    def x_send(t):
-        h, step = t // nx, t % nx
-        at = pl.ds(pl.multiple_of(block_start(t), tj), tj)
+        if t + 1 < nt:
+            count_copy(t + 1).wait()
+        acc = None
+        for g in range(nd):
+            if g + 1 < nd:
+                misfit(t, g + 1)
+            elif t + 1 < nt:
+                misfit(t + 1, 0)
+            acc = add_tall(t, g, acc)
+        dacc[pl.ds(pl.multiple_of(block_start(t), tj), tj), :] = acc.T
+
+    s1, s2, zc, xc = {}, {}, {}, []
+
+    def x_send(h, step):
+        start = block_start(step * nh + h)
         slot = h * (nx - 1) + step
-        c = rc(dacc.at[at, :], r1.at[slot], s1s.at[slot], s1r.at[slot], src=a * nx + lax.rem(b + 1 + step, nx))
-        c.start()
-        s1.append(c)
+        for e in far_first + [0]:
+            at = flip(e) * zrows
+            c = rc(dacc.at[pl.ds(pl.multiple_of(start + at, zrows), zrows), :],
+                   r1.at[slot, pl.ds(pl.multiple_of(at, zrows), zrows), :],
+                   s1s.at[slot * nz + e], s1r.at[slot * nz + e], src=a * nx + lax.rem(b + 1 + step, nx))
+            c.start()
+            s1[slot, e] = c
 
     def z_piece(h, owner):
         return pl.ds(pl.multiple_of(b * half + h * tj + owner * zrows, zrows), zrows)
 
-    def z_send(h):
-        own = pl.ds(pl.multiple_of(b * half + h * tj, tj), tj)
-        value = dacc[own, :]
+    def z_send(h, e):
+        owner = flip(e)
+        at = z_piece(h, owner)
+        value = dacc[at, :]
         for step in range(nx - 1):
-            s1[h * (nx - 1) + step].wait_recv()
-            value = value + r1[h * (nx - 1) + step]
-        dacc[own, :] = value
-        for o in range(1, nz):
-            owner = lax.rem(a + o, nz)
-            slot = h * (nz - 1) + o - 1
-            c = rc(dacc.at[z_piece(h, owner), :], r2.at[slot], s2s.at[slot], s2r.at[slot], src=owner * nx + b)
+            s1[h * (nx - 1) + step, e].wait_recv()
+            value = value + r1[h * (nx - 1) + step, pl.ds(pl.multiple_of(owner * zrows, zrows), zrows), :]
+        dacc[at, :] = value
+        if e:
+            slot = h * (nz - 1) + e - 1
+            c = rc(dacc.at[at, :], r2.at[slot], s2s.at[slot], s2r.at[slot], src=owner * nx + b)
             c.start()
-            s2.append(c)
+            s2[h, e] = c
 
     def x_copy(h, step, o):
-        at = z_piece(h, lax.rem(a - o + nz, nz))
+        at = z_piece(h, flip(o))
         slot = (h * (nx - 1) + step) * nz + o
         return rc(g_dst.at[at, :], g_dst.at[at, :], xs.at[slot], xr.at[slot],
                   src=a * nx + lax.rem(b + 1 + step, nx))
@@ -224,39 +227,37 @@
     def finish(h):
         mine = z_piece(h, a)
         total = dacc[mine, :]
-        for o in range(1, nz):
-            s2[h * (nz - 1) + o - 1].wait_recv()
-            total = total + r2[h * (nz - 1) + o - 1]
+        for e in far_first:
+            s2[h, e].wait_recv()
+            total = total + r2[h * (nz - 1) + e - 1]
         g_dst[mine, :] = total * scale_dst
+        for e in far_first:
+            slot = h * (nz - 1) + e - 1
+            c = rc(g_dst.at[mine, :], g_dst.at[mine, :], zs.at[slot], zr.at[slot], src=flip(e) * nx + b)
+            c.start()
+            zc[h, e] = c
         x_forward(h, 0)
-        for o in range(1, nz):
-            slot = h * (nz - 1) + o - 1
-            c = rc(g_dst.at[mine, :], g_dst.at[mine, :], zs.at[slot], zr.at[slot], src=lax.rem(a + o, nz) * nx + b)
-            c.start()
-            zc[h, o] = c
 
     def forward(h):
-        for o in range(1, nz):
-            zc[h, o].wait_recv()
-            x_forward(h, o)
+        for e in far_first:
+            zc[h, e].wait_recv()
+            x_forward(h, e)
 
     q1c, q2c = [], []
 
-    def last_block(t):
-        start = block_start(t)
+    def project_all():
+        left = far_first + [0]
         gacc = None
+        thr[0] = through(group_of(0))
         for g, (side, oy) in enumerate(groups):
-            slot = g % 2
-            first = group_first(g)
+            first = group_of(g) * kd
             if g + 1 < nd:
-                misfit(t, start, group_first(g + 1), 1 - slot)
-            new = gather_terms(start, first, slot)
-            th, tl = split(new)
+                thr[(g + 1) % 2] = through(group_of(g + 1))
             for e in range(kd):
-                rows = slice(e * ni, (e + 1) * ni)
-                wide = dg(sth, jnp.concatenate([th[rows], tl[rows]], axis=1), 1, 0)
-                proj[first + e] = wide[:, :r2n] + wide[:, r2n:] + dg(stl, th[rows], 1, 0)
-                term = dg(jnp.concatenate([th[rows], tl[rows], th[rows]], axis=1), chs[first + e], 1, 1)
+                th, tl = split(thr[g % 2, e * ni:(e + 1) * ni])
+                wide = dg(sth, jnp.concatenate([th, tl], axis=1), 1, 0)
+                proj[first + e] = wide[:, :r2n] + wide[:, r2n:] + dg(stl, th, 1, 0)
+                term = dg(jnp.concatenate([th, tl, th], axis=1), chs[first + e], 1, 1)
                 gacc = term if gacc is None else gacc + term
             core_of = lax.rem(cc + side, 2)
             peer = lax.rem(yy + oy, ny)
@@ -271,21 +272,24 @@
                     c = rc(q1.at[peer], q2.at[oy - 1], q2s.at[oy - 1], q2r.at[oy - 1], dst=2 * peer + cc)
                     c.start()
                     q2c.append(c)
-            if g == nd // 2 - 1:
+            if g == 0:
                 for h in range(nh - 1):
-                    z_send(h)
+                    for e in far_first + [0]:
+                        z_send(h, e)
+            else:
+                for _ in range(len(left) // (nd - g)):
+                    z_send(nh - 1, left.pop(0))
         gterm[...] = gacc
-        dacc[pl.ds(pl.multiple_of(start, tj), tj), :] = accr[...].T
 
     count_copy(0).wait()
-    misfit(0, block_start(0), 0 if nt > 1 else first_hour, 0)
-    for t in range(nt - 1):
+    misfit(0, 0)
+    for t in range(nt):
         compute_block(t)
         if t == 0:
             pl.semaphore_wait(barrier, n - 1 + nd - 1)
-        if t % nx < nx - 1:
-            x_send(t)
-    last_block(nt - 1)
+        if t // nh < nx - 1:
+            x_send(t % nh, t // nh)
+    project_all()
 
     g1 = []
     for o in range(1, nd):
@@ -295,7 +299,8 @@
         c.start()
         g1.append(c)
 
-    z_send(nh - 1)
+    for h in range(nh - 1):
+        finish(h)
 
     ysum = q1[yy]
     for o in range(1, ny):
@@ -310,9 +315,6 @@
         c.start()
         q3c.append(c)
 
-    for h in range(nh - 1):
-        finish(h)
-
     def hour_row(r, carry):
         for k in range(kk):
             acc = core[r, 0:8, :] * proj[k, 0:8, :]
@@ -357,6 +359,9 @@
         c.start()
         h2.append(c)
 
+    for h in range(nh):
+        forward(h)
+
     psum = pq[s]
     for o in range(1, n):
         q3c[o - 1].wait_recv()
@@ -367,9 +372,6 @@
         c = rc(pk.at[d], pk.at[d], pks.at[o - 1], pkr.at[o - 1], dst=lax.rem(d + o, nd))
         c.start()
         pkc.append(c)
-
-    for h in range(nh):
-        forward(h)
 
     for o in range(1, n):
         h2[o - 1].wait_recv()
@@ -391,7 +393,7 @@
         c.wait_recv()
     for c in xc:
         c.wait_recv()
-    for c in s1 + s2 + list(zc.values()) + xc + g1 + g2 + q1c + q2c + q3c + pkc + h1 + h2:
+    for c in list(s1.values()) + list(s2.values()) + list(zc.values()) + xc + g1 + g2 + q1c + q2c + q3c + pkc + h1 + h2:
         c.wait_send()
 
 
@@ -429,13 +431,13 @@
         scratch = [
             f(ni, r1n), f(nj, r2n), f(r3n, r1n, r2n), pltpu.VMEM((nh * nx, kk, ni, tj), jnp.int32),
             f(kk, r1n, r2n), h(kk, ni, 3 * r2n), h(kk, 2 * r2n, ni), h(3 * r2n, nj), h(nj, 2 * r2n),
-            f(kk, ni, r2n), f(nj, r2n), f(nh * (nx - 1), tj, r2n), f(nh * (nz - 1), tj // nz, r2n),
+            f(2, kd * ni, r2n), f(nj, r2n), f(nh * (nx - 1), tj, r2n), f(nh * (nz - 1), tj // nz, r2n),
             h(kk, r1n, 3 * r2n), f(ni, r1n), f(nd - 1, irows, r1n), f(kk, r1n, r2n), f(ny, kd, r1n, r2n), f(ny - 1, kd, r1n, r2n),
             f(n, kd, share, r2n), f(n - 1, kd, share, r2n), f(nd, kd, share, r2n), f(kk, r3n, 8, r2n),
-            f(nd, kk, 128), f(n, kk, 128), h(2, 2, kd * ni, tj), f(r2n, tj),
+            f(nd, kk, 128), f(n, kk, 128), h(nh * nx, nd, 2, kd * ni, tj),
             dma(3), dma(nh * nx),
         ]
-        for m in (nh * (nx - 1), nh * (nz - 1), nh * (nz - 1), nh * (nx - 1) * nz, nd - 1, nd - 1, ny, ny - 1, n - 1, nd - 1, nd - 1, n - 1):
+        for m in (nh * (nx - 1) * nz, nh * (nz - 1), nh * (nz - 1), nh * (nx - 1) * nz, nd - 1, nd - 1, ny, ny - 1, n - 1, nd - 1, nd - 1, n - 1):
             scratch += pair(m)
         shapes = ((ni, r1n), (nj, r2n), (kk, r3n), (r3n, share, r2n))
         results = pl.pallas_call(

time: 40.9 us -> 40.5 us (level)
  no operation moved by 1% of the time
where the time goes in v2:
time: 40.5 us; the launch traced here: 40.3 us
  Pallas kernels  39.6 us (98%)
  between operations  0.64 us (2%)
    pallas_call x1, Pallas kernels, shards(): pl.pallas_call(functools.partial(kernel, n, nz, nx, nd, nh, tj), out_shap...  38.7 us
    pallas_call x1, Pallas kernels, shards(): pl.pallas_call(write_out, out_shape=tuple((jax.ShapeDtypeStruct(x, F32) f...  0.96 us

profile of v2, /device:TPU:0, one launch (start us, length us, event | category | flops | bytes accessed | tf_op | source)
XLA Modules:
  0.0 40.3 jit_solution(14859910306681292021)
XLA Ops:
  0.6 38.7 %shard_map.84 = (f32[256,128]{1,0:T(8,128)S(1)}, f32[1024,128]{1,0:T(8,128)S(1)}, f32[8,32]{1,0:T(8,128)S(1)}, f32[32,16,128]{2,1,0:T(8,128)S(1)}) custom-call(s32[8,256,1024]{2,1,0:T(8,128)} %counts.1, f32[256,128]{1,0:T(8,128)} %src_in.1, f32[1024,128]{1,0:T(8,128)} %dst_in.1, f32[8,32]{1,0:T(8,128)} %hour.1, f32[32,128,128]{2,1,0:T(8,128)} %core_in.1), custom_call_target="tpu_custom_call" | custom-call | tf_op jit(solution)/shard_map/pallas_call | solution.py:443
  39.3 1.0 %shard_map.85 = (f32[256,128]{1,0:T(8,128)}, f32[1024,128]{1,0:T(8,128)}, f32[8,32]{1,0:T(8,128)}, f32[32,16,128]{2,1,0:T(8,128)}) custom-call(f32[256,128]{1,0:T(8,128)S(1)} %get-tuple-element.8.refs_0_, f32[1024,128]{1,0:T(8,128)S(1)} %get-tuple-element.9.refs_1_, f32[8,32]{1,0:T(8,128)S(1)} %get-tuple-element.10.refs_2_, ...), custom_call_target="tpu_custom_call" | custom-call | tf_op jit(solution)/shard_map/pallas_call | solution.py:453

commit v3 on v2

--- a/solution.py
+++ b/solution.py
@@ -164,7 +164,7 @@
             out = new if out is None else out + new
         return out
 
-    groups = [(side, oy) for side in (1, 0) for oy in list(range(1, ny)) + [0]]
+    groups = [(side, oy) for oy in list(range(1, ny)) + [0] for side in (1, 0)]
 
     def group_of(g):
         side, oy = groups[g]

time: 40.5 us -> 40.5 us (level)
  no operation moved by 1% of the time
where the time goes in v3:
time: 40.5 us; the launch traced here: 40.3 us
  Pallas kernels  39.6 us (98%)
  between operations  0.64 us (2%)
    pallas_call x1, Pallas kernels, shards(): pl.pallas_call(functools.partial(kernel, n, nz, nx, nd, nh, tj), out_shap...  38.7 us
    pallas_call x1, Pallas kernels, shards(): pl.pallas_call(write_out, out_shape=tuple((jax.ShapeDtypeStruct(x, F32) f...  0.96 us

profile of v3, /device:TPU:0, one launch (start us, length us, event | category | flops | bytes accessed | tf_op | source)
XLA Modules:
  0.0 40.3 jit_solution(8151187801362576189)
XLA Ops:
  0.6 38.7 %shard_map.84 = (f32[256,128]{1,0:T(8,128)S(1)}, f32[1024,128]{1,0:T(8,128)S(1)}, f32[8,32]{1,0:T(8,128)S(1)}, f32[32,16,128]{2,1,0:T(8,128)S(1)}) custom-call(s32[8,256,1024]{2,1,0:T(8,128)} %counts.1, f32[256,128]{1,0:T(8,128)} %src_in.1, f32[1024,128]{1,0:T(8,128)} %dst_in.1, f32[8,32]{1,0:T(8,128)} %hour.1, f32[32,128,128]{2,1,0:T(8,128)} %core_in.1), custom_call_target="tpu_custom_call" | custom-call | tf_op jit(solution)/shard_map/pallas_call | solution.py:443
  39.3 1.0 %shard_map.85 = (f32[256,128]{1,0:T(8,128)}, f32[1024,128]{1,0:T(8,128)}, f32[8,32]{1,0:T(8,128)}, f32[32,16,128]{2,1,0:T(8,128)}) custom-call(f32[256,128]{1,0:T(8,128)S(1)} %get-tuple-element.8.refs_0_, f32[1024,128]{1,0:T(8,128)S(1)} %get-tuple-element.9.refs_1_, f32[8,32]{1,0:T(8,128)S(1)} %get-tuple-element.10.refs_2_, ...), custom_call_target="tpu_custom_call" | custom-call | tf_op jit(solution)/shard_map/pallas_call | solution.py:453
